TPU v7x, 32 devices: a whole 2x2x4 slice. The times are simulated.
32 devices in a mesh: dp: 8 (over z, core), mp: 4 (over y, x).
Axes of the slice: x: 2, y: 2, z: 4, core: 2. Of those that a mesh axis runs over, the one named last changes fastest.
Arguments:
- grad_parts: bfloat16 [8, 64, 256, 256], P('dp', 'mp'), may hold values from -0.25 to 0.25
- left_stats: float32 [8, 4, 4, 256, 256], P('dp', 'mp'), may hold values from -6 to 6
- right_stats: float32 [8, 4, 4, 256, 256], P('dp', 'mp'), may hold values from -6 to 6
- left_root: bfloat16 [8, 4, 4, 256, 256], P('dp', 'mp'), may hold values from -4 to 4
- right_root: bfloat16 [8, 4, 4, 256, 256], P('dp', 'mp'), may hold values from -4 to 4
- owners: int32 [64], replicated, may hold values from 0 to 3, as said below
Outputs:
- direction: bfloat16 [64, 256, 256], P('mp')
- left_updated: float32 [8, 4, 4, 256, 256], P('dp', 'mp')
- right_updated: float32 [8, 4, 4, 256, 256], P('dp', 'mp')
Inputs may be any that keep to these rules, and one draw needn't show every extreme that they name: The blocks b with the same b // 2 have distinct owners. Among the blocks of one row, no owner is named more than 4 times, and in every row some owner is named exactly 4 times.
All inputs are finite; a program needn't handle non-finite values.
Results may differ from a plain program's by a relative error of at most 0.02.
Values may be sent and summed in bfloat16 or wider, within the bound.
A program may use at most 64 MiB of HBM per device.

v0:
```python
import jax
import jax.numpy as jnp
from jax import lax
from jax.sharding import PartitionSpec as P


def per_device(grad_parts, left_stats, right_stats, left_root, right_root, owners):
    dp_count = lax.axis_size("dp")
    mp_count = lax.axis_size("mp")
    dp_index = lax.axis_index("dp")
    mp_index = lax.axis_index("mp")
    per_shard = grad_parts.shape[1]
    held_count = per_shard // dp_count
    slots_count = left_stats.shape[2]
    total_blocks = owners.shape[0]
    block_ids = jnp.arange(total_blocks, dtype=jnp.int32)
    row_of = block_ids % per_shard // held_count
    same_owner = owners[:, None] == owners[None, :]
    before = block_ids[None, :] < block_ids[:, None]
    slot_of = jnp.sum(
        ((row_of[:, None] == row_of[None, :]) & same_owner & before).astype(jnp.int32), axis=1
    )
    row_pos = jnp.arange(mp_count * held_count, dtype=jnp.int32)
    row_ids = row_pos // held_count * per_shard + dp_index * held_count + row_pos % held_count
    row_owner = jnp.take(owners, row_ids)
    row_slot = jnp.take(slot_of, row_ids)
    slot_ids = jnp.arange(slots_count, dtype=jnp.int32)
    mine_in = (row_owner[None, :] == mp_index) & (row_slot[None, :] == slot_ids[:, None])
    local_ids = (
        mp_index * per_shard + dp_index * held_count + jnp.arange(held_count, dtype=jnp.int32)
    )
    local_owner = jnp.take(owners, local_ids)
    summed = lax.psum(grad_parts[0], "dp").astype(jnp.float32)
    shares = lax.dynamic_slice_in_dim(summed, dp_index * held_count, held_count, 0)
    held_blocks = shares.astype(jnp.bfloat16)
    targets = jnp.arange(mp_count, dtype=jnp.int32)
    send_map = (local_owner[None, :] == targets[:, None]).astype(jnp.bfloat16)
    row_holder = row_pos // held_count
    receive_map = jnp.any(
        mine_in[:, :, None] & (row_holder[None, :, None] == targets[None, None, :]), axis=1
    ).astype(jnp.bfloat16)
    packed = jnp.einsum(
        "qj,jxy->qxy", send_map, held_blocks, preferred_element_type=jnp.float32
    ).astype(jnp.bfloat16)
    arrived = lax.all_to_all(packed, "mp", split_axis=0, concat_axis=0, tiled=True)
    owned_grad = jnp.einsum(
        "sq,qxy->sxy", receive_map, arrived, preferred_element_type=jnp.float32
    ).astype(jnp.bfloat16)
    left_updated = left_stats[0, 0] + jnp.einsum(
        "sik,sjk->sij", owned_grad, owned_grad, preferred_element_type=jnp.float32
    )
    right_updated = right_stats[0, 0] + jnp.einsum(
        "ski,skj->sij", owned_grad, owned_grad, preferred_element_type=jnp.float32
    )
    half_step = jnp.einsum(
        "sik,skj->sij", left_root[0, 0], owned_grad, preferred_element_type=jnp.float32
    ).astype(jnp.bfloat16)
    precond = jnp.einsum(
        "sik,skj->sij", half_step, right_root[0, 0], preferred_element_type=jnp.float32
    ).astype(jnp.bfloat16)
    out_packed = jnp.einsum(
        "sq,sxy->qxy", receive_map, precond, preferred_element_type=jnp.float32
    ).astype(jnp.bfloat16)
    came_back = lax.all_to_all(out_packed, "mp", split_axis=0, concat_axis=0, tiled=True)
    returned = jnp.einsum(
        "qj,qxy->jxy", send_map, came_back, preferred_element_type=jnp.float32
    ).astype(jnp.bfloat16)
    direction = lax.all_gather(returned, "dp", axis=0, tiled=True)
    return (direction, left_updated[None, None], right_updated[None, None])


def solution(mesh):
    in_specs = (
        P("dp", "mp", None, None),
        P("dp", "mp", None, None, None),
        P("dp", "mp", None, None, None),
        P("dp", "mp", None, None, None),
        P("dp", "mp", None, None, None),
        P(),
    )
    out_specs = (
        P("mp", None, None),
        P("dp", "mp", None, None, None),
        P("dp", "mp", None, None, None),
    )
    return jax.shard_map(
        per_device, mesh=mesh, in_specs=in_specs, out_specs=out_specs, check_vma=False
    )
```

profile of v0, /device:TPU:0, one launch (start us, length us, event | category | flops | bytes accessed | tf_op | source)
XLA Modules:
  0.0 142.9 jit_solution(12366330903584625655)
XLA Ops:
  7.2 0.0 copy-start
  7.2 0.0 all-reduce.2.cloned.1.call-start
  7.2 4.1 %copy.61 = bf16[1,16,256,256]{3,1,2,0:T(8,128)(2,1)} copy(bf16[1,16,256,256]{3,2,1,0:T(8,128)(2,1)} %param.8) | data formatting | bytes 4194304 | tf_op args[0]
  11.4 0.0 copy-start.1
  11.4 0.0 all-reduce.2.cloned.1.call-update
  11.4 0.6 copy-done.1
  12.0 0.2 convert_reduce_fusion
  12.2 0.6 gather_fusion.1
  12.9 0.6 gather_fusion.2
  13.5 0.6 gather_fusion
  14.2 65.2 %all-reduce.2.cloned.1.call-done = bf16[16,256,256]{2,0,1:T(8,128)(2,1)} async-done(((bf16[16,256,256]{2,0,1:T(8,128)(2,1)}), bf16[16,256,256]{2,0,1:T(8,128)(2,1)}) %all-reduce.2.cloned.1.call-update) | async-done | bytes 2097168 | tf_op jit(solution)/shard_map/psum | solution.py:33
  79.4 1.8 %convolution_convert_fusion.4 = bf16[4,256,256]{2,0,1:T(4,128)(2,1)S(1)} fusion(bf16[16,256,256]{2,0,1:T(8,128)(2,1)} %all-reduce.2.cloned.1.call-done, s32[]{:T(128)S(6)} %select_n.90, s32[2]{0:T(128)S(1)} %and_select_fusion.4), kind=kOutput, calls=%fused_computation.12 | convolution fusion | flops 1572872 | bytes 786444 | tf_op jit(solution)/shard_map/qj,jxy->qxy/dot_general | solution.py:42
  81.2 0.0 copy-start.3
  81.2 0.9 copy.34
  82.1 3.6 %all-to-all-start = ((bf16[4,256,256]{2,1,0:T(8,128)(2,1)}), bf16[4,256,256]{2,1,0:T(8,128)(2,1)S(1)}, u32[]{:S(2)}, u32[]{:S(2)}) async-start(bf16[4,256,256]{2,1,0:T(8,128)(2,1)} %copy.34), calls=%async_computation | async-start | bytes 1048576 | tf_op jit(solution)/shard_map/all_to_all | solution.py:45
  85.8 0.0 all-gather.2.cloned.1.call-start
  85.8 0.2 and_reduce_fusion
  85.9 6.5 %all-to-all-done = bf16[4,256,256]{2,1,0:T(8,128)(2,1)S(1)} async-done(((bf16[4,256,256]{2,1,0:T(8,128)(2,1)}), bf16[4,256,256]{2,1,0:T(8,128)(2,1)S(1)}, u32[]{:S(2)}, u32[]{:S(2)}) %all-to-all-start) | async-done | bytes 524320 | tf_op jit(solution)/shard_map/all_to_all | solution.py:45
  92.5 0.5 convolution_convert_fusion.3
  93.0 0.3 copy.36
  93.3 0.0 copy-done
  93.3 0.0 copy-done.3
  93.3 0.6 convolution_convert_fusion.1
  93.9 0.6 convolution_convert_fusion
  94.5 0.1 copy.40
  94.6 9.7 %all_to_all.10 = bf16[4,256,256]{2,1,0:T(8,128)(2,1)S(1)} all-to-all(bf16[4,256,256]{2,1,0:T(8,128)(2,1)S(1)} %copy.40), channel_id=1, replica_groups=mesh['dp'=8,'mp'=4] {'mp'}, dimensions={0} | all-to-all | bytes 1048576 | tf_op jit(solution)/shard_map/all_to_all | solution.py:64
  104.3 0.0 copy-start.2
  104.3 0.5 convolution_convert_fusion.5
  104.8 0.7 copy.42
  105.5 0.0 all-gather.2.cloned.1.call-update
  105.6 2.5 %fusion.1 = f32[1,1,4,256,256]{4,3,2,1,0:T(8,128)} fusion(f32[1,1,4,256,256]{4,3,2,1,0:T(8,128)} %param.9, bf16[4,256,256]{2,0,1:T(4,128)(2,1)S(1)} %convolution_convert_fusion.3), kind=kOutput, calls=%fused_computation.7 | convolution fusion | flops 134479872 | bytes 2621440 | tf_op jit(solution)/shard_map/sik,sjk->sij/dot_general | solution.py:49
  108.1 0.0 copy-done.2
  108.1 1.3 fusion
  109.4 23.6 %all-gather.2.cloned.1.call-done = bf16[16,256,256]{2,1,0:T(8,128)(2,1)} async-done(((bf16[2,256,256]{2,1,0:T(8,128)(2,1)}), bf16[16,256,256]{2,1,0:T(8,128)(2,1)}) %all-gather.2.cloned.1.call-update) | async-done | bytes 2097168 | tf_op jit(solution)/shard_map/all_gather | solution.py:68
  132.9 3.1 %copy.64 = bf16[16,256,256]{2,1,0:T(8,128)(2,1)} copy(bf16[16,256,256]{2,1,0:T(8,128)(2,1)} %all-gather.2.cloned.1.call-done) | data formatting | bytes 4194304
  (11 shorter events, 0.1 us)
Async XLA Ops:
  7.2 86.1 %copy-start = (bf16[1,1,4,256,256]{4,3,2,1,0:T(8,128)(2,1)S(1)}, bf16[1,1,4,256,256]{4,3,2,1,0:T(8,128)(2,1)}, u32[]{:S(2)}) copy-start(bf16[1,1,4,256,256]{4,3,2,1,0:T(8,128)(2,1)} %param.12) | copy-start | bytes 1572868
  7.2 72.2 %all-reduce.2.cloned.1.call-start = ((), (), s32[]{:S(2)}) async-start(), calls=%async_computation.2 | async-start | bytes 4194304 | tf_op jit(solution)/shard_map/psum | solution.py:33
  11.4 0.7 copy-start.1
  81.2 12.1 %copy-start.3 = (bf16[1,1,4,256,256]{4,3,2,1,0:T(8,128)(2,1)S(1)}, bf16[1,1,4,256,256]{4,3,2,1,0:T(8,128)(2,1)}, u32[]{:S(2)}) copy-start(bf16[1,1,4,256,256]{4,3,2,1,0:T(8,128)(2,1)} %param.11) | copy-start | bytes 1572868
  82.1 10.3 %all-to-all-start = ((bf16[4,256,256]{2,1,0:T(8,128)(2,1)}), bf16[4,256,256]{2,1,0:T(8,128)(2,1)S(1)}, u32[]{:S(2)}, u32[]{:S(2)}) async-start(bf16[4,256,256]{2,1,0:T(8,128)(2,1)} %copy.34), calls=%async_computation | async-start | bytes 1048576 | tf_op jit(solution)/shard_map/all_to_all | solution.py:45
  85.8 47.2 %all-gather.2.cloned.1.call-start = ((), (), s32[]{:S(2)}) async-start(), calls=%async_computation.3 | async-start | bytes 2359296 | tf_op jit(solution)/shard_map/all_gather | solution.py:68
  104.3 3.9 %copy-start.2 = (f32[1,1,4,256,256]{4,3,2,1,0:T(8,128)S(1)}, f32[1,1,4,256,256]{4,3,2,1,0:T(8,128)}, u32[]{:S(2)}) copy-start(f32[1,1,4,256,256]{4,3,2,1,0:T(8,128)} %param.10) | copy-start | bytes 3145732
Sparse Core Ops, SparseCore 0:
  11.5 67.8 all-reduce.1
  105.7 27.2 all-gather.1
where the time goes:
time: 143 us
  waiting for transfers between devices  95.3 us (67%)
  between operations  14.2 us (10%)
  local copies, waits for them, and re-layouts  11.8 us (8%)
  blocking collectives  9.67 us (7%)
  matrix products  7.86 us (5%)
  starting transfers between devices  3.69 us (3%)
    psum x1, waiting for transfers between devices, per_device(): summed = lax.psum(grad_parts[0], 'dp').astype(jnp.float32)  65.2 us
    all_gather x1, waiting for transfers between devices, per_device(): direction = lax.all_gather(returned, 'dp', axis=0, tiled=True)  23.6 us
    all_to_all x1, blocking collectives, per_device(): lax.all_to_all(out_packed, 'mp', split_axis=0, concat_axis=0, tiled=True)  9.67 us
    unnamed x10, local copies, waits for them, and re-layouts  7.84 us
    all_to_all x1, waiting for transfers between devices, per_device(): lax.all_to_all(packed, 'mp', split_axis=0, concat_axis=0, tiled=True)  6.52 us
    all_to_all x1, starting transfers between devices, per_device(): lax.all_to_all(packed, 'mp', split_axis=0, concat_axis=0, tiled=True)  3.65 us
  transfers between devices with their start and end apart: 3, of which 3 were waited for; matrix products, arithmetic and copies ran while one was open for 4% of the time, Pallas kernels for 0%

commit v1 on v0

v1 whole, which is shorter than its diff:
```python
import functools

import jax
import jax.numpy as jnp
from jax import lax
from jax.experimental import pallas as pl
from jax.experimental.pallas import tpu as pltpu
from jax.sharding import PartitionSpec as P

CORES = 2
MESH = pl.DeviceIdType.MESH
F32, BF16 = jnp.float32, jnp.bfloat16


def kernel(
    n, mp, held, slots,
    owners, grads, left_in, right_in, lroot_in, rroot_in,
    dir_out, left_out, right_out,
    own, part, partial, recv, accf, gbuf, pack, arrived, owned, prec, backp, came, dirbuf,
    lstat, rstat, lroot, rroot, back_sel,
    own_sem, part_send, part_recv, red_send, red_recv, fwd_send, fwd_recv, back_send, back_recv,
    gat_send, gat_recv, pair_send, pair_recv, write_sem, stat_sem,
):
    dp, me = lax.axis_index("dp"), lax.axis_index("mp")
    z, c = dp // CORES, dp % CORES
    partner = dp + 1 - 2 * c
    per = n * CORES * held

    def loop(count, body):
        def step(i, carry):
            body(i)
            return carry
        lax.fori_loop(0, count, step, 0)

    def own_copy(d):
        return pltpu.make_async_copy(
            grads.at[0, pl.ds((d * CORES + c) * held, held)],
            own.at[pl.ds(d * held, held)], own_sem.at[d])

    stat_copies = [
        pltpu.make_async_copy(lroot_in.at[0, 0], lroot, stat_sem.at[0]),
        pltpu.make_async_copy(rroot_in.at[0, 0], rroot, stat_sem.at[1]),
        pltpu.make_async_copy(left_in.at[0, 0], lstat, stat_sem.at[2]),
        pltpu.make_async_copy(right_in.at[0, 0], rstat, stat_sem.at[3]),
    ]
    loop(n, lambda d: own_copy(d).start())

    barrier = pltpu.get_barrier_semaphore()
    pl.semaphore_signal(barrier, inc=1, device_id={"dp": partner, "mp": me}, device_id_type=MESH)

    @pl.when(z > 0)
    def _():
        pl.semaphore_signal(barrier, inc=1, device_id={"dp": dp - CORES, "mp": me}, device_id_type=MESH)

    @pl.when(z < n - 1)
    def _():
        pl.semaphore_signal(barrier, inc=1, device_id={"dp": dp + CORES, "mp": me}, device_id_type=MESH)

    for k in range(1, mp):
        pl.semaphore_signal(
            barrier, inc=1, device_id={"dp": dp, "mp": lax.rem(me + k, mp)}, device_id_type=MESH)
    neighbours = jnp.where(z > 0, 1, 0) + jnp.where(z < n - 1, 1, 0)
    pl.semaphore_wait(barrier, mp + neighbours)

    def part_copy(d):
        return pltpu.make_async_remote_copy(
            src_ref=grads.at[0, pl.ds((d * CORES + 1 - c) * held, held)],
            dst_ref=part.at[pl.ds(d * held, held)],
            send_sem=part_send.at[d], recv_sem=part_recv.at[d],
            device_id={"dp": partner, "mp": me}, device_id_type=MESH)

    toward = jnp.where(2 * z < n, 1, -1)

    def far_first(t, sign):
        return jnp.where(sign > 0, n - 1 - t, t)

    loop(n, lambda t: part_copy(far_first(t, toward)).start())
    for copy in stat_copies:
        copy.start()

    def red_copy(d, j, sign, lane):
        i = d * held + j
        return pltpu.make_async_remote_copy(
            src_ref=partial.at[i], dst_ref=recv.at[lane, i],
            send_sem=red_send.at[i], recv_sem=red_recv.at[lane, i],
            device_id={"dp": dp + CORES * sign, "mp": me}, device_id_type=MESH)

    def both(d):
        own_copy(d).wait()
        part_copy(d).wait_recv()

    def red_step(t):
        for stream in range(2):
            sign = toward if stream == 0 else -toward
            lane = jnp.where(sign > 0, 0, 1)
            d = far_first(t, sign)
            before = z - sign

            @pl.when((d - z) * sign > 0)
            def _():
                both(d)

                def block(j):
                    i = d * held + j
                    has = (before >= 0) & (before < n)

                    @pl.when(has)
                    def _():
                        red_copy(d, j, sign, lane).wait_recv()
                        partial[i] = (
                            own[i].astype(F32) + part[i].astype(F32) + recv[lane, i].astype(F32)
                        ).astype(BF16)

                    @pl.when(jnp.logical_not(has))
                    def _():
                        partial[i] = (own[i].astype(F32) + part[i].astype(F32)).astype(BF16)

                    red_copy(d, j, sign, lane).start()

                loop(held, block)

    loop(n - 1, red_step)

    my_owner = [owners[me * per + dp * held + j] for j in range(held)]

    def held_for(q):
        pick = jnp.int32(0)
        for j in range(held):
            pick = jnp.where(my_owner[j] == q, j, pick)
        return pick

    count = jnp.int32(0)
    source = [jnp.int32(0)] * slots
    filled = [jnp.int32(0)] * slots
    for q in range(mp):
        slot_for_q = jnp.int32(0)
        for j in range(held):
            mine = owners[q * per + dp * held + j] == me
            for s in range(slots):
                hit = mine & (count == s)
                source[s] = jnp.where(hit, q, source[s])
                filled[s] = jnp.where(hit, 1, filled[s])
                slot_for_q = jnp.where(hit, s, slot_for_q)
            count = count + mine.astype(jnp.int32)
        back_sel[q] = slot_for_q

    both(z)

    def finish(j):
        i = z * held + j
        accf[...] = own[i].astype(F32) + part[i].astype(F32)

        @pl.when(z > 0)
        def _():
            red_copy(z, j, 1, 0).wait_recv()
            accf[...] += recv[0, i].astype(F32)

        @pl.when(z < n - 1)
        def _():
            red_copy(z, j, -1, 1).wait_recv()
            accf[...] += recv[1, i].astype(F32)

        gbuf[j] = accf[...].astype(BF16)

    loop(held, finish)

    def exchange(src, dst, sends, recvs, k):
        return pltpu.make_async_remote_copy(
            src_ref=src.at[k], dst_ref=dst.at[me],
            send_sem=sends.at[k], recv_sem=recvs.at[k],
            device_id={"dp": dp, "mp": lax.rem(me + k, mp)}, device_id_type=MESH)

    def send_held(t):
        k = mp - 1 - t
        pack[k] = gbuf[held_for(lax.rem(me + k, mp))]
        exchange(pack, arrived, fwd_send, fwd_recv, k).start()

    loop(mp - 1, send_held)
    arrived[me] = gbuf[held_for(me)]
    for copy in stat_copies[:2]:
        copy.wait()
    loop(mp - 1, lambda t: exchange(pack, arrived, fwd_send, fwd_recv, t + 1).wait_recv())

    def dot(a, b, dims=((1,), (0,))):
        return lax.dot_general(a, b, (dims, ((), ())), preferred_element_type=F32)

    for s in range(slots):
        block = arrived[source[s]]
        owned[s] = jnp.where(filled[s] > 0, block.astype(F32), 0.0).astype(BF16)
    for s in range(slots):
        half = dot(lroot[s], owned[s]).astype(BF16)
        prec[s] = dot(half, rroot[s]).astype(BF16)

    def send_back(t):
        k = mp - 1 - t
        backp[k] = prec[back_sel[lax.rem(me + k, mp)]]
        exchange(backp, came, back_send, back_recv, k).start()

    loop(mp - 1, send_back)
    came[me] = prec[back_sel[me]]

    for copy in stat_copies[2:]:
        copy.wait()
    for s in range(slots):
        lstat[s] += dot(owned[s], owned[s], ((1,), (1,)))
        rstat[s] += dot(owned[s], owned[s], ((0,), (0,)))
    stat_writes = [
        pltpu.make_async_copy(lstat, left_out.at[0, 0], stat_sem.at[4]),
        pltpu.make_async_copy(rstat, right_out.at[0, 0], stat_sem.at[5]),
    ]
    for copy in stat_writes:
        copy.start()
    loop(mp - 1, lambda t: exchange(backp, came, back_send, back_recv, t + 1).wait_recv())
    for j in range(held):
        dirbuf[dp * held + j] = came[my_owner[j]]

    def gat_copy(r, j, sign, lane):
        i = (r * CORES + c) * held + j
        return pltpu.make_async_remote_copy(
            src_ref=dirbuf.at[i], dst_ref=dirbuf.at[i],
            send_sem=gat_send.at[lane, r * held + j], recv_sem=gat_recv.at[r * held + j],
            device_id={"dp": dp + CORES * sign, "mp": me}, device_id_type=MESH)

    def pair_copy(r, j, core):
        i = (r * CORES + core) * held + j
        return pltpu.make_async_remote_copy(
            src_ref=dirbuf.at[i], dst_ref=dirbuf.at[i],
            send_sem=pair_send.at[r * held + j], recv_sem=pair_recv.at[r * held + j],
            device_id={"dp": partner, "mp": me}, device_id_type=MESH)

    def write(r, core):
        i = (r * CORES + core) * held
        return pltpu.make_async_copy(
            dirbuf.at[pl.ds(i, held)], dir_out.at[pl.ds(i, held)],
            write_sem.at[r * CORES + core])

    def first(j):
        @pl.when(z < n - 1)
        def _():
            gat_copy(z, j, 1, 0).start()

        @pl.when(z > 0)
        def _():
            gat_copy(z, j, -1, 1).start()

        pair_copy(z, j, c).start()

    loop(held, first)
    write(z, c).start()

    def gather_step(t):
        for lane, sign in ((0, 1), (1, -1)):
            r = z - sign * (t + 1)
            after = z + sign

            @pl.when((r >= 0) & (r < n))
            def _():
                def block(j):
                    gat_copy(r, j, sign, lane).wait_recv()

                    @pl.when((after >= 0) & (after < n))
                    def _():
                        gat_copy(r, j, sign, lane).start()

                    pair_copy(r, j, c).start()

                loop(held, block)
                write(r, c).start()

    loop(n - 1, gather_step)

    def pair_row(r):
        loop(held, lambda j: pair_copy(r, j, 1 - c).wait_recv())
        write(r, 1 - c).start()

    pair_row(z)

    def pair_step(t):
        for sign in (1, -1):
            r = z - sign * (t + 1)

            @pl.when((r >= 0) & (r < n))
            def _():
                pair_row(r)

    loop(n - 1, pair_step)

    def drain(r):
        part_copy(r).wait_send()
        write(r, 0).wait()
        write(r, 1).wait()

        def block(j):
            pair_copy(r, j, c).wait_send()

            @pl.when(r != z)
            def _():
                red_copy(r, j, 1, 0).wait_send()

            @pl.when((r <= z) & (z < n - 1))
            def _():
                gat_copy(r, j, 1, 0).wait_send()

            @pl.when((r >= z) & (z > 0))
            def _():
                gat_copy(r, j, -1, 1).wait_send()

        loop(held, block)

    loop(n, drain)

    def drain_exchange(t):
        exchange(pack, arrived, fwd_send, fwd_recv, t + 1).wait_send()
        exchange(backp, came, back_send, back_recv, t + 1).wait_send()

    loop(mp - 1, drain_exchange)
    for copy in stat_writes:
        copy.wait()


def per_device(n_dp, mp, grad_parts, left_stats, right_stats, left_root, right_root, owners):
    n = n_dp // CORES
    per, (rows, cols) = grad_parts.shape[1], grad_parts.shape[2:]
    held, slots = per // n_dp, left_stats.shape[2]
    hbm = pl.BlockSpec(memory_space=pltpu.HBM)

    def blocks(*lead, kind=BF16):
        return pltpu.VMEM((*lead, rows, cols), kind)

    dma = pltpu.SemaphoreType.DMA
    return pl.pallas_call(
        functools.partial(kernel, n, mp, held, slots),
        out_shape=(
            jax.ShapeDtypeStruct((per, rows, cols), BF16),
            jax.ShapeDtypeStruct(left_stats.shape, F32),
            jax.ShapeDtypeStruct(right_stats.shape, F32),
        ),
        in_specs=[pl.BlockSpec(memory_space=pltpu.SMEM)] + [hbm] * 5,
        out_specs=(hbm, hbm, hbm),
        scratch_shapes=[
            blocks(n * held), blocks(n * held), blocks(n * held), blocks(2, n * held),
            blocks(kind=F32), blocks(held), blocks(mp), blocks(mp), blocks(slots), blocks(slots),
            blocks(mp), blocks(mp), blocks(per),
            blocks(slots, kind=F32), blocks(slots, kind=F32), blocks(slots), blocks(slots),
            pltpu.SMEM((mp,), jnp.int32),
            dma((n,)), dma((n,)), dma((n,)), dma((n * held,)), dma((2, n * held)),
            dma((mp,)), dma((mp,)), dma((mp,)), dma((mp,)),
            dma((2, n * held)), dma((n * held,)), dma((n * held,)), dma((n * held,)),
            dma((n_dp,)), dma((6,)),
        ],
        compiler_params=pltpu.CompilerParams(
            collective_id=0, has_side_effects=True),
    )(owners, grad_parts, left_stats, right_stats, left_root, right_root)


def solution(mesh):
    five = P("dp", "mp", None, None, None)
    return jax.shard_map(
        functools.partial(per_device, mesh.shape["dp"], mesh.shape["mp"]),
        mesh=mesh,
        in_specs=(P("dp", "mp", None, None), five, five, five, five, P()),
        out_specs=(P("mp", None, None), five, five),
        check_vma=False,
    )
```

time: 143 us -> 67.1 us (0.47)
  waiting for transfers between devices: 95.3 us -> 0 us
  Pallas kernels: 0 us -> 60.6 us
  between operations: 14.2 us -> 0.66 us
  blocking collectives: 9.67 us -> 0 us
  matrix products: 7.86 us -> 0 us
  local copies, waits for them, and re-layouts: 11.8 us -> 5.19 us
  starting transfers between devices: 3.69 us -> 0 us
    psum x1 -> x0, waiting for transfers between devices: 65.2 us -> none  [per_device(): summed = lax.psum(grad_parts[0], 'dp').astype(jnp.float32)]
    pallas_call x0 -> x1, Pallas kernels: none -> 60.6 us  [per_device(): pl.pallas_call(functools.partial(kernel, n, mp, held, slots), out_shape=(...]
    all_gather x1 -> x0, waiting for transfers between devices: 23.6 us -> none  [per_device(): direction = lax.all_gather(returned, 'dp', axis=0, tiled=True)]
    all_to_all x1 -> x0, blocking collectives: 9.67 us -> none  [per_device(): lax.all_to_all(out_packed, 'mp', split_axis=0, concat_axis=0, tiled=True)]
    dot_general x7 -> x0, matrix products: 7.86 us -> none  [the longest x1 2.54 us: per_device(): jnp.einsum('sik,sjk->sij', owned_grad, owned_grad, preferred_element_type...]
    all_to_all x1 -> x0, waiting for transfers between devices: 6.52 us -> none  [per_device(): lax.all_to_all(packed, 'mp', split_axis=0, concat_axis=0, tiled=True)]
    all_to_all x1 -> x0, starting transfers between devices: 3.65 us -> none  [per_device(): lax.all_to_all(packed, 'mp', split_axis=0, concat_axis=0, tiled=True)]
    unnamed x10 -> x7, local copies, waits for them, and re-layouts: 7.84 us -> 5.19 us
  transfers between devices with their start and end apart: 3 -> 0, of which waited for: 3 -> 0; matrix products, arithmetic and copies ran while one was open for 4% -> 0% of each run, Pallas kernels for 0% -> 0%
where the time goes in v1:
time: 67.1 us; the launch traced here: 66.4 us
  Pallas kernels  60.6 us (90%)
  local copies, waits for them, and re-layouts  5.19 us (8%)
    pallas_call x1, Pallas kernels, per_device(): pl.pallas_call(functools.partial(kernel, n, mp, held, slots), out_shape=(...  60.6 us
    unnamed x7, local copies, waits for them, and re-layouts  5.19 us

profile of v1, /device:TPU:0, one launch (start us, length us, event | category | flops | bytes accessed | tf_op | source)
XLA Modules:
  0.0 66.4 jit_solution(9583221905662102120)
XLA Ops:
  0.6 60.6 %shard_map.85 = (bf16[16,256,256]{2,1,0:T(8,128)(2,1)}, f32[1,1,4,256,256]{4,3,2,1,0:T(8,128)}, f32[1,1,4,256,256]{4,3,2,1,0:T(8,128)}) custom-call(s32[64]{0:T(128)} %owners.1, bf16[1,16,256,256]{3,2,1,0:T(8,128)(2,1)} %grads.1, f32[1,1,4,256,256]{4,3,2,1,0:T(8,128)} %left_in.1, f32[1,1,4,256,256]{4,3,2,1,0:T(8,128)} %right_in.1, ...), custom_call_target="tpu_custom_call" | custom-call | tf_op jit(solution)/shard_map/pallas_call | solution.py:331
  61.2 0.0 copy-start.1
  61.2 0.0 copy-start
  61.2 3.2 %copy.12 = bf16[16,256,256]{2,1,0:T(8,128)(2,1)} copy(bf16[16,256,256]{2,1,0:T(8,128)(2,1)} %get-tuple-element.6) | data formatting | bytes 4194304
  64.5 0.0 copy-done.1
  64.5 1.0 %copy.13 = f32[1,1,4,256,256]{4,3,2,1,0:T(8,128)} copy(f32[1,1,4,256,256]{4,3,2,1,0:T(8,128)S(1)} %copy-done.1) | data formatting | bytes 2097152
  65.4 0.0 copy-done
  65.4 1.0 %copy.14 = f32[1,1,4,256,256]{4,3,2,1,0:T(8,128)} copy(f32[1,1,4,256,256]{4,3,2,1,0:T(8,128)S(1)} %copy-done) | data formatting | bytes 2097152
Async XLA Ops:
  61.2 3.3 %copy-start.1 = (f32[1,1,4,256,256]{4,3,2,1,0:T(8,128)S(1)}, f32[1,1,4,256,256]{4,3,2,1,0:T(8,128)}, u32[]{:S(2)}) copy-start(f32[1,1,4,256,256]{4,3,2,1,0:T(8,128)} %get-tuple-element.7) | copy-start | bytes 3145732
  61.2 4.2 %copy-start = (f32[1,1,4,256,256]{4,3,2,1,0:T(8,128)S(1)}, f32[1,1,4,256,256]{4,3,2,1,0:T(8,128)}, u32[]{:S(2)}) copy-start(f32[1,1,4,256,256]{4,3,2,1,0:T(8,128)} %get-tuple-element.8) | copy-start | bytes 3145732

commit v2 on v1

--- a/solution.py
+++ b/solution.py
@@ -19,7 +19,7 @@
     own, part, partial, recv, accf, gbuf, pack, arrived, owned, prec, backp, came, dirbuf,
     lstat, rstat, lroot, rroot, back_sel,
     own_sem, part_send, part_recv, red_send, red_recv, fwd_send, fwd_recv, back_send, back_recv,
-    gat_send, gat_recv, pair_send, pair_recv, write_sem, stat_sem,
+    gat_send, gat_recv, pair_send, pair_recv, write_sem, stat_sem, turn_sem,
 ):
     dp, me = lax.axis_index("dp"), lax.axis_index("mp")
     z, c = dp // CORES, dp % CORES
@@ -119,7 +119,22 @@
 
                 loop(held, block)
 
+    @pl.when(c == 1)
+    def _():
+        pl.semaphore_wait(turn_sem, 1)
+
     loop(n - 1, red_step)
+
+    def sums_left(d):
+        @pl.when(d != z)
+        def _():
+            loop(held, lambda j: red_copy(d, j, 1, 0).wait_send())
+
+    @pl.when(c == 0)
+    def _():
+        loop(n, sums_left)
+        pl.semaphore_signal(
+            turn_sem, inc=1, device_id={"dp": partner, "mp": me}, device_id_type=MESH)
 
     my_owner = [owners[me * per + dp * held + j] for j in range(held)]
 
@@ -293,7 +308,7 @@
         def block(j):
             pair_copy(r, j, c).wait_send()
 
-            @pl.when(r != z)
+            @pl.when((r != z) & (c == 1))
             def _():
                 red_copy(r, j, 1, 0).wait_send()
 
@@ -346,7 +361,7 @@
             dma((n,)), dma((n,)), dma((n,)), dma((n * held,)), dma((2, n * held)),
             dma((mp,)), dma((mp,)), dma((mp,)), dma((mp,)),
             dma((2, n * held)), dma((n * held,)), dma((n * held,)), dma((n * held,)),
-            dma((n_dp,)), dma((6,)),
+            dma((n_dp,)), dma((6,)), pltpu.SemaphoreType.REGULAR,
         ],
         compiler_params=pltpu.CompilerParams(
             collective_id=0, has_side_effects=True),

time: 67.1 us -> 63.9 us (0.952)
  Pallas kernels: 60.6 us -> 57.9 us
    pallas_call x1, Pallas kernels: 60.6 us -> 57.9 us  [per_device(): pl.pallas_call(functools.partial(kernel, n, mp, held, slots), out_shape=(...]
where the time goes in v2:
time: 63.9 us; the launch traced here: 63.8 us
  Pallas kernels  57.9 us (91%)
  local copies, waits for them, and re-layouts  5.19 us (8%)
  between operations  0.66 us (1%)
    pallas_call x1, Pallas kernels, per_device(): pl.pallas_call(functools.partial(kernel, n, mp, held, slots), out_shape=(...  57.9 us
    unnamed x7, local copies, waits for them, and re-layouts  5.19 us

profile of v2, /device:TPU:0, one launch (start us, length us, event | category | flops | bytes accessed | tf_op | source)
XLA Modules:
  0.0 63.8 jit_solution(10624703938417021828)
XLA Ops:
  0.6 57.9 %shard_map.85 = (bf16[16,256,256]{2,1,0:T(8,128)(2,1)}, f32[1,1,4,256,256]{4,3,2,1,0:T(8,128)}, f32[1,1,4,256,256]{4,3,2,1,0:T(8,128)}) custom-call(s32[64]{0:T(128)} %owners.1, bf16[1,16,256,256]{3,2,1,0:T(8,128)(2,1)} %grads.1, f32[1,1,4,256,256]{4,3,2,1,0:T(8,128)} %left_in.1, f32[1,1,4,256,256]{4,3,2,1,0:T(8,128)} %right_in.1, ...), custom_call_target="tpu_custom_call" | custom-call | tf_op jit(solution)/shard_map/pallas_call | solution.py:346
  58.6 0.0 copy-start.1
  58.6 0.0 copy-start
  58.6 3.2 %copy.12 = bf16[16,256,256]{2,1,0:T(8,128)(2,1)} copy(bf16[16,256,256]{2,1,0:T(8,128)(2,1)} %get-tuple-element.6) | data formatting | bytes 4194304
  61.8 0.0 copy-done.1
  61.8 1.0 %copy.13 = f32[1,1,4,256,256]{4,3,2,1,0:T(8,128)} copy(f32[1,1,4,256,256]{4,3,2,1,0:T(8,128)S(1)} %copy-done.1) | data formatting | bytes 2097152
  62.8 0.0 copy-done
  62.8 1.0 %copy.14 = f32[1,1,4,256,256]{4,3,2,1,0:T(8,128)} copy(f32[1,1,4,256,256]{4,3,2,1,0:T(8,128)S(1)} %copy-done) | data formatting | bytes 2097152
Async XLA Ops:
  58.6 3.3 %copy-start.1 = (f32[1,1,4,256,256]{4,3,2,1,0:T(8,128)S(1)}, f32[1,1,4,256,256]{4,3,2,1,0:T(8,128)}, u32[]{:S(2)}) copy-start(f32[1,1,4,256,256]{4,3,2,1,0:T(8,128)} %get-tuple-element.7) | copy-start | bytes 3145732
  58.6 4.2 %copy-start = (f32[1,1,4,256,256]{4,3,2,1,0:T(8,128)S(1)}, f32[1,1,4,256,256]{4,3,2,1,0:T(8,128)}, u32[]{:S(2)}) copy-start(f32[1,1,4,256,256]{4,3,2,1,0:T(8,128)} %get-tuple-element.8) | copy-start | bytes 3145732

commit v3 on v2

--- a/solution.py
+++ b/solution.py
@@ -14,12 +14,12 @@
 
 def kernel(
     n, mp, held, slots,
-    owners, grads, left_in, right_in, lroot_in, rroot_in,
-    dir_out, left_out, right_out,
-    own, part, partial, recv, accf, gbuf, pack, arrived, owned, prec, backp, came, dirbuf,
-    lstat, rstat, lroot, rroot, back_sel,
+    owners_in, grads, left_in, right_in, lroot_in, rroot_in,
+    dirbuf, lstat, rstat,
+    own, part, partial, recv, accf, gbuf, pack, arrived, owned, prec, backp, came,
+    lroot, rroot, owners, back_sel,
     own_sem, part_send, part_recv, red_send, red_recv, fwd_send, fwd_recv, back_send, back_recv,
-    gat_send, gat_recv, pair_send, pair_recv, write_sem, stat_sem, turn_sem,
+    gat_send, gat_recv, pair_send, pair_recv, stat_sem, turn_sem,
 ):
     dp, me = lax.axis_index("dp"), lax.axis_index("mp")
     z, c = dp // CORES, dp % CORES
@@ -40,9 +40,11 @@
     stat_copies = [
         pltpu.make_async_copy(lroot_in.at[0, 0], lroot, stat_sem.at[0]),
         pltpu.make_async_copy(rroot_in.at[0, 0], rroot, stat_sem.at[1]),
-        pltpu.make_async_copy(left_in.at[0, 0], lstat, stat_sem.at[2]),
-        pltpu.make_async_copy(right_in.at[0, 0], rstat, stat_sem.at[3]),
+        pltpu.make_async_copy(left_in, lstat, stat_sem.at[2]),
+        pltpu.make_async_copy(right_in, rstat, stat_sem.at[3]),
     ]
+    owners_copy = pltpu.make_async_copy(owners_in, owners, stat_sem.at[4])
+    owners_copy.start()
     loop(n, lambda d: own_copy(d).start())
 
     barrier = pltpu.get_barrier_semaphore()
@@ -136,6 +138,7 @@
         pl.semaphore_signal(
             turn_sem, inc=1, device_id={"dp": partner, "mp": me}, device_id_type=MESH)
 
+    owners_copy.wait()
     my_owner = [owners[me * per + dp * held + j] for j in range(held)]
 
     def held_for(q):
@@ -217,14 +220,8 @@
     for copy in stat_copies[2:]:
         copy.wait()
     for s in range(slots):
-        lstat[s] += dot(owned[s], owned[s], ((1,), (1,)))
-        rstat[s] += dot(owned[s], owned[s], ((0,), (0,)))
-    stat_writes = [
-        pltpu.make_async_copy(lstat, left_out.at[0, 0], stat_sem.at[4]),
-        pltpu.make_async_copy(rstat, right_out.at[0, 0], stat_sem.at[5]),
-    ]
-    for copy in stat_writes:
-        copy.start()
+        lstat[0, 0, s] += dot(owned[s], owned[s], ((1,), (1,)))
+        rstat[0, 0, s] += dot(owned[s], owned[s], ((0,), (0,)))
     loop(mp - 1, lambda t: exchange(backp, came, back_send, back_recv, t + 1).wait_recv())
     for j in range(held):
         dirbuf[dp * held + j] = came[my_owner[j]]
@@ -243,12 +240,6 @@
             send_sem=pair_send.at[r * held + j], recv_sem=pair_recv.at[r * held + j],
             device_id={"dp": partner, "mp": me}, device_id_type=MESH)
 
-    def write(r, core):
-        i = (r * CORES + core) * held
-        return pltpu.make_async_copy(
-            dirbuf.at[pl.ds(i, held)], dir_out.at[pl.ds(i, held)],
-            write_sem.at[r * CORES + core])
-
     def first(j):
         @pl.when(z < n - 1)
         def _():
@@ -261,7 +252,6 @@
         pair_copy(z, j, c).start()
 
     loop(held, first)
-    write(z, c).start()
 
     def gather_step(t):
         for lane, sign in ((0, 1), (1, -1)):
@@ -280,13 +270,11 @@
                     pair_copy(r, j, c).start()
 
                 loop(held, block)
-                write(r, c).start()
 
     loop(n - 1, gather_step)
 
     def pair_row(r):
         loop(held, lambda j: pair_copy(r, j, 1 - c).wait_recv())
-        write(r, 1 - c).start()
 
     pair_row(z)
 
@@ -302,8 +290,6 @@
 
     def drain(r):
         part_copy(r).wait_send()
-        write(r, 0).wait()
-        write(r, 1).wait()
 
         def block(j):
             pair_copy(r, j, c).wait_send()
@@ -329,7 +315,14 @@
         exchange(backp, came, back_send, back_recv, t + 1).wait_send()
 
     loop(mp - 1, drain_exchange)
-    for copy in stat_writes:
+
+
+def write_out(*refs):
+    sources, targets, sem = refs[:3], refs[3:6], refs[6]
+    copies = [pltpu.make_async_copy(sources[i], targets[i], sem.at[i]) for i in range(3)]
+    for copy in copies:
+        copy.start()
+    for copy in copies:
         copy.wait()
 
 
@@ -343,29 +336,41 @@
         return pltpu.VMEM((*lead, rows, cols), kind)
 
     dma = pltpu.SemaphoreType.DMA
-    return pl.pallas_call(
+    results = (
+        pltpu.VMEM((per, rows, cols), BF16),
+        pltpu.VMEM(left_stats.shape, F32),
+        pltpu.VMEM(right_stats.shape, F32),
+    )
+    operands = [
+        pltpu.with_memory_space_constraint(x, pltpu.HBM)
+        for x in (owners, grad_parts, left_stats, right_stats, left_root, right_root)
+    ]
+    held_on_chip = pl.pallas_call(
         functools.partial(kernel, n, mp, held, slots),
-        out_shape=(
-            jax.ShapeDtypeStruct((per, rows, cols), BF16),
-            jax.ShapeDtypeStruct(left_stats.shape, F32),
-            jax.ShapeDtypeStruct(right_stats.shape, F32),
-        ),
-        in_specs=[pl.BlockSpec(memory_space=pltpu.SMEM)] + [hbm] * 5,
-        out_specs=(hbm, hbm, hbm),
+        out_shape=results,
+        in_specs=[hbm] * 6,
+        out_specs=[pl.BlockSpec(memory_space=pltpu.VMEM)] * 3,
         scratch_shapes=[
             blocks(n * held), blocks(n * held), blocks(n * held), blocks(2, n * held),
             blocks(kind=F32), blocks(held), blocks(mp), blocks(mp), blocks(slots), blocks(slots),
-            blocks(mp), blocks(mp), blocks(per),
-            blocks(slots, kind=F32), blocks(slots, kind=F32), blocks(slots), blocks(slots),
-            pltpu.SMEM((mp,), jnp.int32),
+            blocks(mp), blocks(mp), blocks(slots), blocks(slots),
+            pltpu.SMEM(owners.shape, jnp.int32), pltpu.SMEM((mp,), jnp.int32),
             dma((n,)), dma((n,)), dma((n,)), dma((n * held,)), dma((2, n * held)),
             dma((mp,)), dma((mp,)), dma((mp,)), dma((mp,)),
             dma((2, n * held)), dma((n * held,)), dma((n * held,)), dma((n * held,)),
-            dma((n_dp,)), dma((6,)), pltpu.SemaphoreType.REGULAR,
+            dma((5,)), pltpu.SemaphoreType.REGULAR,
         ],
         compiler_params=pltpu.CompilerParams(
-            collective_id=0, has_side_effects=True),
-    )(owners, grad_parts, left_stats, right_stats, left_root, right_root)
+            collective_id=0, has_side_effects=True, vmem_limit_bytes=32 * 1024 * 1024),
+    )(*operands)
+    return pl.pallas_call(
+        write_out,
+        out_shape=[jax.ShapeDtypeStruct(x.shape, x.dtype) for x in held_on_chip],
+        in_specs=[pl.BlockSpec(memory_space=pltpu.VMEM)] * 3,
+        out_specs=[hbm] * 3,
+        scratch_shapes=[dma((3,))],
+        compiler_params=pltpu.CompilerParams(vmem_limit_bytes=1024 * 1024),
+    )(*held_on_chip)
 
 
 def solution(mesh):

time: 63.9 us -> 59.4 us (0.930)
  local copies, waits for them, and re-layouts: 5.19 us -> 0 us
  Pallas kernels: 57.9 us -> 58.6 us
    unnamed x7 -> x0, local copies, waits for them, and re-layouts: 5.19 us -> none
    pallas_call x1 -> x2, Pallas kernels: 57.9 us -> 58.6 us  [the longest x1 56.6 us: per_device(): pl.pallas_call(functools.partial(kernel, n, mp, held, slots), out_shape=r...]
where the time goes in v3:
time: 59.4 us; the launch traced here: 59.2 us
  Pallas kernels  58.6 us (99%)
  between operations  0.64 us (1%)
    pallas_call x1, Pallas kernels, per_device(): pl.pallas_call(functools.partial(kernel, n, mp, held, slots), out_shape=r...  56.6 us
    pallas_call x1, Pallas kernels, per_device(): pl.pallas_call(write_out, out_shape=[jax.ShapeDtypeStruct(x.shape, x.dtyp...  2.03 us

profile of v3, /device:TPU:0, one launch (start us, length us, event | category | flops | bytes accessed | tf_op | source)
XLA Modules:
  0.0 59.2 jit_solution(17751669898819084606)
XLA Ops:
  0.6 56.6 %shard_map.85 = (bf16[16,256,256]{2,1,0:T(8,128)(2,1)S(1)}, f32[1,1,4,256,256]{4,3,2,1,0:T(8,128)S(1)}, f32[1,1,4,256,256]{4,3,2,1,0:T(8,128)S(1)}) custom-call(s32[64]{0:T(128)} %owners_in.1, bf16[1,16,256,256]{3,2,1,0:T(8,128)(2,1)} %grads.1, f32[1,1,4,256,256]{4,3,2,1,0:T(8,128)} %left_in.1, f32[1,1,4,256,256]{4,3,2,1,0:T(8,128)} %right_in.1, ...), custom_call_target="tpu_custom_call" | custom-call | tf_op jit(solution)/shard_map/pallas_call | solution.py:348
  57.2 2.0 %shard_map.86 = (bf16[16,256,256]{2,1,0:T(8,128)(2,1)}, f32[1,1,4,256,256]{4,3,2,1,0:T(8,128)}, f32[1,1,4,256,256]{4,3,2,1,0:T(8,128)}) custom-call(bf16[16,256,256]{2,1,0:T(8,128)(2,1)S(1)} %get-tuple-element.6.refs_0_, f32[1,1,4,256,256]{4,3,2,1,0:T(8,128)S(1)} %get-tuple-element.7.refs_1_, f32[1,1,4,256,256]{4,3,2,1,0:T(8,128)S(1)} %get-tuple-element.8.refs_2_), custom_call_target="tpu_custom_call" | custom-call | tf_op jit(solution)/shard_map/pallas_call | solution.py:366

commit v4 on v3

--- a/solution.py
+++ b/solution.py
@@ -127,10 +127,18 @@
 
     loop(n - 1, red_step)
 
+    def last_sum(d, j):
+        return (d == z + toward) & (j == held - 1)
+
     def sums_left(d):
         @pl.when(d != z)
         def _():
-            loop(held, lambda j: red_copy(d, j, 1, 0).wait_send())
+            def block(j):
+                @pl.when(jnp.logical_not(last_sum(d, j)))
+                def _():
+                    red_copy(d, j, 1, 0).wait_send()
+
+            loop(held, block)
 
     @pl.when(c == 0)
     def _():
@@ -205,9 +213,10 @@
     for s in range(slots):
         block = arrived[source[s]]
         owned[s] = jnp.where(filled[s] > 0, block.astype(F32), 0.0).astype(BF16)
+    halves = [dot(lroot[s], owned[s]).astype(BF16) for s in range(slots)]
+    steps = [dot(halves[s], rroot[s]).astype(BF16) for s in range(slots)]
     for s in range(slots):
-        half = dot(lroot[s], owned[s]).astype(BF16)
-        prec[s] = dot(half, rroot[s]).astype(BF16)
+        prec[s] = steps[s]
 
     def send_back(t):
         k = mp - 1 - t
@@ -221,7 +230,6 @@
         copy.wait()
     for s in range(slots):
         lstat[0, 0, s] += dot(owned[s], owned[s], ((1,), (1,)))
-        rstat[0, 0, s] += dot(owned[s], owned[s], ((0,), (0,)))
     loop(mp - 1, lambda t: exchange(backp, came, back_send, back_recv, t + 1).wait_recv())
     for j in range(held):
         dirbuf[dp * held + j] = came[my_owner[j]]
@@ -252,6 +260,8 @@
         pair_copy(z, j, c).start()
 
     loop(held, first)
+    for s in range(slots):
+        rstat[0, 0, s] += dot(owned[s], owned[s], ((0,), (0,)))
 
     def gather_step(t):
         for lane, sign in ((0, 1), (1, -1)):
@@ -294,7 +304,7 @@
         def block(j):
             pair_copy(r, j, c).wait_send()
 
-            @pl.when((r != z) & (c == 1))
+            @pl.when((r != z) & ((c == 1) | last_sum(r, j)))
             def _():
                 red_copy(r, j, 1, 0).wait_send()
 

time: 59.4 us -> 60 us (1.010)
  Pallas kernels: 58.6 us -> 59.2 us
where the time goes in v4:
time: 60 us; the launch traced here: 59.8 us
  Pallas kernels  59.2 us (99%)
  between operations  0.64 us (1%)
    pallas_call x1, Pallas kernels, per_device(): pl.pallas_call(functools.partial(kernel, n, mp, held, slots), out_shape=r...  57.1 us
    pallas_call x1, Pallas kernels, per_device(): pl.pallas_call(write_out, out_shape=[jax.ShapeDtypeStruct(x.shape, x.dtyp...  2.03 us

profile of v4, /device:TPU:0, one launch (start us, length us, event | category | flops | bytes accessed | tf_op | source)
XLA Modules:
  0.0 59.8 jit_solution(16090982432919992684)
XLA Ops:
  0.6 57.1 %shard_map.85 = (bf16[16,256,256]{2,1,0:T(8,128)(2,1)S(1)}, f32[1,1,4,256,256]{4,3,2,1,0:T(8,128)S(1)}, f32[1,1,4,256,256]{4,3,2,1,0:T(8,128)S(1)}) custom-call(s32[64]{0:T(128)} %owners_in.1, bf16[1,16,256,256]{3,2,1,0:T(8,128)(2,1)} %grads.1, f32[1,1,4,256,256]{4,3,2,1,0:T(8,128)} %left_in.1, f32[1,1,4,256,256]{4,3,2,1,0:T(8,128)} %right_in.1, ...), custom_call_target="tpu_custom_call" | custom-call | tf_op jit(solution)/shard_map/pallas_call | solution.py:358
  57.8 2.0 %shard_map.86 = (bf16[16,256,256]{2,1,0:T(8,128)(2,1)}, f32[1,1,4,256,256]{4,3,2,1,0:T(8,128)}, f32[1,1,4,256,256]{4,3,2,1,0:T(8,128)}) custom-call(bf16[16,256,256]{2,1,0:T(8,128)(2,1)S(1)} %get-tuple-element.6.refs_0_, f32[1,1,4,256,256]{4,3,2,1,0:T(8,128)S(1)} %get-tuple-element.7.refs_1_, f32[1,1,4,256,256]{4,3,2,1,0:T(8,128)S(1)} %get-tuple-element.8.refs_2_), custom_call_target="tpu_custom_call" | custom-call | tf_op jit(solution)/shard_map/pallas_call | solution.py:376
